TPU v7x, 32 devices: a whole 2x2x4 slice. The times are simulated.
32 devices in a mesh: gx: 4 (over y, core), gy: 2 (over x), gz: 4 (over z).
Axes of the slice: x: 2, y: 2, z: 4, core: 2. Of those that a mesh axis runs over, the one named last changes fastest.
Arguments:
- density: float32 [32, 32, 512], P('gx', 'gy', 'gz'), may hold values from 0.7 to 1.6
- momentum: float32 [32, 32, 512], P('gx', 'gy', 'gz'), may hold values from -7 to 7
- hydrogen: float32 [32, 32, 512], P('gx', 'gy', 'gz'), may hold values from 0.05 to 1.2
- forced_modes: int32 [96, 3], replicated, may hold values from -3 to 3, as said below
Outputs:
- density_rate: float32 [32, 32, 512], P('gx', 'gy', 'gz')
- momentum_rate: float32 [32, 32, 512], P('gx', 'gy', 'gz')
- hydrogen_rate: float32 [32, 32, 512], P('gx', 'gy', 'gz')
Inputs may be any that keep to these rules, and one draw needn't show every extreme that they name: `forced_modes`: each row is a wave vector (kx, ky, kz) with 1 <= kx^2 + ky^2 + kz^2 <= 9; the 96 rows are distinct.
All inputs are finite; a program needn't handle non-finite values.
Results may differ from a plain program's by a relative error of at most 0.0003.
Values sent between devices are 32-bit elements; how exact they have to be, the bound alone decides.
A program may use at most 64 MiB of HBM per device.

v0:
```python
import functools
import math

import jax
import jax.numpy as jnp
import numpy as np
from jax import lax
from jax.experimental import pallas as pl
from jax.experimental.pallas import tpu as pltpu
from jax.sharding import PartitionSpec as P

KMAX = 3
WIDTH = 2 * KMAX + 1
HALF = 64
ROWS = KMAX + 1
REACH = 4
LOAD_PLANES = 4

FIRST_COEFFS = (0.8, -0.2, 4.0 / 105.0, -1.0 / 280.0)
SECOND_COEFFS = (1.6, -0.2, 8.0 / 315.0, -1.0 / 560.0)
CENTRE_COEFF = -205.0 / 72.0
VISCOSITY = 0.3
DIFFUSIVITY = 1.5
FORCE_POWER = 0.3
ENERGY_EPS = 1e-06
ACTIVATION = 2.0
HIGHEST = lax.Precision.HIGHEST
MESH = pl.DeviceIdType.MESH


def packed_modes():
    reach = range(-KMAX, KMAX + 1)
    cells = [(x, y, z) for z in range(ROWS) for x in reach for y in reach
             if x * x + y * y + z * z <= KMAX * KMAX and (z, x, y) > (0, 0, 0)]
    return cells


def packed_index(place):
    cells = packed_modes()
    result = []
    for part in range(3):
        value = jnp.full(place.shape, cells[0][part], jnp.int32)
        if part == 1:
            value = value + place
        for i in range(1, len(cells)):
            step = cells[i][part] - cells[i - 1][part] - (part == 1)
            if step:
                value = value + jnp.where(place >= i, step, 0)
        result.append(value)
    return result


def tables(size_z):
    band = np.zeros((size_z, size_z))
    halo = np.zeros((16, size_z))
    for z in range(size_z):
        band[z, z] = 3.0 * CENTRE_COEFF
        for offset, weight in enumerate(SECOND_COEFFS, 1):
            for q in (z - offset, z + offset):
                if 0 <= q < size_z:
                    band[q, z] = weight
                elif q < 0:
                    halo[8 + q, z] = weight
                else:
                    halo[8 + q - size_z, z] = weight
    return np.concatenate([halo, band], 0).astype(np.float32)


def polynomial(x, coeffs):
    result = coeffs[-1]
    for c in reversed(coeffs[:-1]):
        result = result * x + c
    return result


SIN_COEFFS = [(-1) ** n * (math.pi / 2) ** (2 * n + 1) / math.factorial(2 * n + 1) for n in range(5)]
COS_COEFFS = [(-1) ** n * (math.pi / 2) ** (2 * n) / math.factorial(2 * n) for n in range(6)]


def cos_sin(quarters):
    turns = jnp.floor(quarters + 0.5)
    d = quarters - turns
    square = d * d
    s = d * polynomial(square, SIN_COEFFS)
    c = polynomial(square, COS_COEFFS)
    half = jnp.floor(0.5 * turns)
    odd = turns - 2.0 * half
    turned = half - 2.0 * jnp.floor(0.5 * half)
    sin_sign = 1.0 - 2.0 * turned
    cos_sign = sin_sign - 2.0 * odd * sin_sign
    swap = odd > 0.5
    return jnp.where(swap, s, c) * cos_sign, jnp.where(swap, c, s) * sin_sign


def split(x):
    high = x.astype(jnp.bfloat16).astype(jnp.float32)
    return high, x - high


def dot_split(a, b, contract):
    return lax.dot_general(a.astype(jnp.bfloat16), b.astype(jnp.bfloat16), (contract, ((), ())),
                           preferred_element_type=jnp.float32)


def column_sum(x):
    x = tree_sum([x[i : i + 8] for i in range(0, x.shape[0], 8)])
    return jnp.sum(x, axis=0, keepdims=True)


def dot_nt(a, b):
    return lax.dot_general(a, b, (((1,), (1,)), ((), ())), precision=HIGHEST, preferred_element_type=jnp.float32)


def dot_nn(a, b):
    return lax.dot_general(a, b, (((1,), (0,)), ((), ())), precision=HIGHEST, preferred_element_type=jnp.float32)


def dot_tn(a, b):
    return lax.dot_general(a, b, (((0,), (0,)), ((), ())), precision=HIGHEST, preferred_element_type=jnp.float32)


def tree_sum(parts):
    parts = list(parts)
    while len(parts) > 1:
        parts = [sum(parts[i : i + 2][1:], parts[i]) for i in range(0, len(parts), 2)]
    return parts[0]


def root_places(sizes):
    places = [(0, 0), (1, 0), (1, max(0, sizes["gz"] // 2 - 1))]
    return [{"gx": x, "gy": 0, "gz": z} for i, (x, z) in enumerate(places) if (x, z) not in places[:i]]


def kernel(sizes, local, dens_hbm, mom_hbm, fuel_hbm, modes_hbm, late_hbm,
           drate, mrate, hrate,
           f, modes, late, cells, along, along_low, across, across_low, edges, sides, ypack, zpack, ztile, own_sum, got_sums, full_sum,
           load_sem, send_sem, halo_recv, z_recv, sum_recv, z_ready, measure):
    size_x, size_y, size_z = local
    rows = size_x * size_y
    me = {a: lax.axis_index(a) for a in sizes}
    count_x, count_y, count_z = sizes["gx"], sizes["gy"], sizes["gz"]
    total = count_x * count_y * count_z
    roots = root_places(sizes)
    rank_of = lambda p: (p["gz"] * count_x + p["gx"]) * count_y + p["gy"]
    rank = rank_of(me)
    root_ranks = [rank_of(r) for r in roots]
    is_root = functools.reduce(jnp.logical_or, [rank == r for r in root_ranks])

    def place_of(i):
        if isinstance(i, int):
            x, y, z = i // count_y % count_x, i % count_y, i // (count_x * count_y)
            return {"gx": jnp.int32(x), "gy": jnp.int32(y), "gz": jnp.int32(z)}
        return {"gx": lax.rem(lax.div(i, count_y), count_x), "gy": lax.rem(i, count_y),
                "gz": lax.div(i, count_x * count_y)}

    def shifted(axis, step):
        return {axis: lax.rem(me[axis] + step % sizes[axis], sizes[axis])}

    own = pl.ds(REACH, size_x)
    load_late = pltpu.make_async_copy(late_hbm, late, load_sem.at[1])
    for at in range(0, size_x, LOAD_PLANES):
        for i, src in enumerate((dens_hbm, mom_hbm)):
            pltpu.make_async_copy(
                src.at[pl.ds(at, LOAD_PLANES)], f.at[i, pl.ds(REACH + at, LOAD_PLANES)], load_sem.at[0]).start()
    load_fuel = pltpu.make_async_copy(fuel_hbm, f.at[2, own], load_sem.at[1])
    load_modes = pltpu.make_async_copy(modes_hbm, modes, load_sem.at[2])

    barrier = pltpu.get_barrier_semaphore()
    z_steps = (1, -1)
    z_next = [shifted("gz", step)["gz"] for step in z_steps]
    z_lower = [z < me["gz"] for z in z_next]
    y_steps = (1, -1) if count_y > 2 else (1,)
    sides_used = len(y_steps)

    def greet(place):
        pl.semaphore_signal(barrier, inc=1, device_id=place, device_id_type=MESH)

    for step in (1, -1):
        greet(shifted("gx", step))
    for step in y_steps:
        greet(shifted("gy", step))
    for step, lower in zip(z_steps, z_lower):
        @pl.when(jnp.logical_not(lower))
        def _(step=step):
            greet(shifted("gz", step))

    @pl.when(is_root)
    def _():
        def greet_one(i, carry):
            @pl.when(i != rank)
            def _():
                greet(place_of(i))
            return carry
        lax.fori_loop(0, total, greet_one, 0)

    greeters = 2 + sides_used + len(roots) - is_root.astype(jnp.int32)
    for lower in z_lower:
        greeters = greeters + lower.astype(jnp.int32)

    lane = lax.broadcasted_iota(jnp.int32, (1, 2 * HALF), 1)
    kx, ky, kz = packed_index(lax.rem(lane, HALF))
    quarter = (lane >= HALF).astype(jnp.float32)
    kx, ky, kz = [k.astype(jnp.float32) for k in (kx, ky, kz)]

    def quarters(k, place, axis, size):
        part = k * place.astype(jnp.float32) / (size * sizes[axis])
        return 4.0 * (part - jnp.floor(part))

    shift = quarters(kz, me["gz"] * size_z, "gz", size_z) - quarter
    rows_y = me["gy"] * size_y + lax.broadcasted_iota(jnp.int32, (size_y, 1), 0)
    angle_y = quarters(ky, rows_y, "gy", size_y) + shift
    for x in range(size_x):
        c, s = cos_sin(angle_y + quarters(kx, me["gx"] * size_x + x, "gx", size_x))
        cells[x * size_y : (x + 1) * size_y, 0 : 2 * HALF] = c
        cells[x * size_y : (x + 1) * size_y, 2 * HALF : 4 * HALF] = -s
    for z in range(0, size_z, 16):
        rows_at = z + lax.broadcasted_iota(jnp.int32, (16, 1), 0)
        for i, x in enumerate(cos_sin(quarters(kz, rows_at, "gz", size_z))):
            high, rest = split(x)
            along[z : z + 16, 2 * HALF * i : 2 * HALF * (i + 1)] = high.astype(jnp.bfloat16)
            along_low[z : z + 16, 2 * HALF * i : 2 * HALF * (i + 1)] = rest.astype(jnp.bfloat16)

    load_fuel.start()
    load_late.start()
    load_modes.start()
    both_loaded = f.at[pl.ds(0, 2), own]
    pltpu.make_async_copy(both_loaded, both_loaded, load_sem.at[0]).wait()
    flat = lambda i: f[i, own].reshape(rows, size_z)
    high, rest = split(flat(1) / flat(0))
    part = dot_split(jnp.concatenate([high, rest], 1), jnp.concatenate([along[...], along[...]], 0), ((1,), (0,)))
    part = part * cells[...] + dot_split(high, along_low[...], ((1,), (0,))) * cells[...]
    cube = column_sum(part[:, 0 : 2 * HALF] + part[:, 2 * HALF : 4 * HALF])
    own_sum[...] = cube
    got_sums[rank] = cube

    pl.semaphore_wait(barrier, greeters)
    def copy_out(src, dst, recv, place):
        return pltpu.make_async_remote_copy(
            src_ref=src, dst_ref=dst, send_sem=send_sem, recv_sem=recv, device_id=place, device_id_type=MESH)

    def spread(i):
        return copy_out(full_sum, full_sum, sum_recv, place_of(i))

    for r in root_ranks:
        @pl.when(rank != r)
        def _(r=r):
            copy_out(own_sum, got_sums.at[rank], sum_recv, place_of(r)).start()

    for step, lower in zip(z_steps, z_lower):
        @pl.when(lower)
        def _(step=step):
            pl.semaphore_signal(z_ready, inc=1, device_id=shifted("gz", step), device_id_type=MESH)

    both_loaded = measure.at[pl.ds(0, (fuel_hbm.size + late_hbm.size) // 1024)]
    pltpu.make_async_copy(both_loaded, both_loaded, load_sem.at[1]).wait()
    halos_x = [
        copy_out(f.at[:, pl.ds(size_x, REACH)], f.at[:, pl.ds(0, REACH)], halo_recv, shifted("gx", 1)),
        copy_out(f.at[:, pl.ds(REACH, REACH)], f.at[:, pl.ds(size_x + REACH, REACH)], halo_recv,
                 shifted("gx", -1)),
    ]
    for copy in halos_x:
        copy.start()
    band_at = 16
    pieces = []
    for i in range(2):
        ypack[i, :, 0:REACH] = f[1 + i, own, 0:REACH]
        ypack[i, :, REACH : 2 * REACH] = f[1 + i, own, size_y - REACH : size_y]
        high, rest = split(flat(1 + i))
        pieces += [high, *split(rest)]
    place = lax.broadcasted_iota(jnp.int32, (8, size_z), 0)
    place = jnp.where(place < REACH, place, place + size_z - 2 * REACH)
    edge = (lax.broadcasted_iota(jnp.int32, (8, size_z), 1) == place).astype(jnp.float32)
    ends = dot_split(edge, jnp.concatenate(pieces, 0), ((1,), (1,)))
    for i in range(2):
        zpack[i] = tree_sum([ends[:, (3 * i + j) * rows : (3 * i + j + 1) * rows] for j in range(3)])
    halos_y = [copy_out(ypack, sides.at[i], halo_recv, shifted("gy", step)) for i, step in enumerate(y_steps)]
    halos_z = [copy_out(zpack, ztile.at[i], z_recv, shifted("gz", step)) for i, step in enumerate(z_steps)]
    for copy, lower in zip(halos_z, z_lower):
        @pl.when(lower)
        def _(copy=copy):
            copy.start()
    for copy in halos_y:
        copy.start()

    lap = [dot_nn(flat(1 + i), late[band_at : band_at + size_z]).reshape(size_x, size_y, size_z) for i in range(2)]
    outs = (drate, mrate, hrate)
    mrate[...] = lap[0]
    hrate[...] = lap[1]

    load_modes.wait()
    count = modes.shape[1]
    code = (modes[0:1] * WIDTH + modes[1:2]) * WIDTH + modes[2:3]
    place = lax.rem(lax.broadcasted_iota(jnp.int32, (2 * HALF, 1), 0), HALF)
    px, py, pz = packed_index(place)
    mine = (px * WIDTH + py) * WIDTH + pz
    used = place < len(packed_modes())
    both_ways = jnp.where(used & (mine == code), 1.0, 0.0) + jnp.where(used & (mine == -code), 1.0, 0.0)
    chosen = dot_nt(jnp.ones((8, count), jnp.float32), both_ways)[0:1]

    ncell = float(rows * size_z * total)
    gain = chosen * (2.0 * FORCE_POWER / ncell)
    for i in range(2):
        here = pl.ds(2 * HALF * i, 2 * HALF)
        across[here] = along[:, here].astype(jnp.float32).T.astype(jnp.bfloat16)
        across_low[here] = along_low[:, here].astype(jnp.float32).T.astype(jnp.bfloat16)

    arrived = [f.at[:, pl.ds(0, 2 * REACH)], sides.at[pl.ds(0, sides_used)]]
    higher = sum(jnp.logical_not(lower).astype(jnp.int32) for lower in z_lower)

    @pl.when(higher > 0)
    def _():
        pl.semaphore_wait(z_ready, higher)

    for copy, lower in zip(halos_z, z_lower):
        @pl.when(jnp.logical_not(lower))
        def _(copy=copy):
            copy.start()

    pltpu.make_async_copy(measure, measure, halo_recv).wait()
    for i in range(2):
        edges[i, :, 0:8] = sides[0, i]
        edges[i, :, 8 : 8 + size_y] = f[1 + i, own]
        edges[i, :, 8 + size_y : 16 + size_y] = sides[sides_used - 1, i]
        total_y = outs[1 + i][...]
        for offset, weight in enumerate(SECOND_COEFFS, 1):
            total_y = total_y + weight * (
                edges[i, :, 8 + offset : 8 + offset + size_y] + edges[i, :, 8 - offset : 8 - offset + size_y])
        outs[1 + i][...] = total_y

    def planes(x, offset):
        return x[REACH + offset : REACH + offset + size_x]

    def first_diff(x):
        result = None
        for offset, weight in enumerate(FIRST_COEFFS, 1):
            term = weight * (planes(x, offset) - planes(x, -offset))
            result = term if result is None else result + term
        return result

    def second_diff(x):
        return tree_sum([w * (planes(x, o) + planes(x, -o)) for o, w in enumerate(SECOND_COEFFS, 1)])

    mom = f[1]
    dens = f[0]
    fuel = f[2]
    vel_pad = mom / dens
    drate[...] = -first_diff(mom)
    mid_fuel = planes(fuel, 0)
    hrate[...] = (DIFFUSIVITY * (hrate[...] + second_diff(fuel)) - first_diff(fuel * vel_pad)
                  - mid_fuel * jnp.exp(-ACTIVATION * mid_fuel / planes(dens, 0)))
    mrate[...] = VISCOSITY * (mrate[...] + second_diff(mom)) - first_diff(mom * vel_pad + dens)

    pltpu.make_async_copy(ztile, ztile, z_recv).wait()
    for i, rate in enumerate((VISCOSITY, DIFFUSIVITY)):
        tile = jnp.concatenate([ztile[0, i], ztile[1, i]], 0)
        outs[1 + i][...] = outs[1 + i][...] + rate * dot_tn(tile, late[0:16]).reshape(size_x, size_y, size_z)

    leaves = [i for i in range(total) if i not in root_ranks]

    @pl.when(is_root)
    def _():
        got = got_sums.at[pl.ds(0, total - 1)]
        pltpu.make_async_copy(got, got, sum_recv).wait()
        full_sum[...] = tree_sum([got_sums[i] for i in range(total)])

    if leaves:
        @pl.when(rank == root_ranks[-1])
        def _():
            for i in reversed(leaves):
                spread(i).start()

        @pl.when(jnp.logical_not(is_root))
        def _():
            pltpu.make_async_copy(full_sum, full_sum, sum_recv).wait()

    cube = full_sum[...]
    coef = cube / ncell
    energy = jnp.sum(chosen * coef * coef, axis=1, keepdims=True)
    scale = 1.0 / (energy + ENERGY_EPS)
    lit = gain * cube
    high, rest = split(cells[...] * jnp.concatenate([lit, lit], 1))
    both = dot_split(high, jnp.concatenate([across[...], across_low[...]], 1), ((1,), (0,)))
    weight = flat(0) * scale
    low = weight * (both[:, 0:size_z] + both[:, size_z:]) + weight * dot_split(rest, across[...], ((1,), (0,)))
    mrate[...] = mrate[...] + low.reshape(size_x, size_y, size_z)

    for sent in (arrived[0], arrived[1], ztile.at[:, :]):
        pltpu.make_async_copy(sent, sent, send_sem).wait()
    for r in root_ranks:
        @pl.when(rank != r)
        def _():
            pltpu.make_async_copy(own_sum, own_sum, send_sem).wait()
    if leaves:
        @pl.when(rank == root_ranks[-1])
        def _():
            sent = got_sums.at[pl.ds(0, len(leaves))]
            pltpu.make_async_copy(sent, sent, send_sem).wait()


def write_out(*refs):
    count = len(refs) // 2
    copies = [pltpu.make_async_copy(refs[i], refs[count + i], refs[-1]) for i in range(count)]
    for copy in copies:
        copy.start()
    for copy in copies:
        copy.wait()


def solution(mesh):
    sizes = {a: mesh.shape[a] for a in ("gx", "gy", "gz")}

    def per_device(density, momentum, hydrogen, forced_modes):
        local = density.shape
        size_x, size_y, size_z = local
        rows = size_x * size_y
        late = tables(size_z)
        modes = forced_modes.T
        total = math.prod(sizes.values())
        halo_bytes = 4 * (3 * 2 * REACH * size_y + (1 + (sizes["gy"] > 2)) * 2 * size_x * 8) * size_z
        any_spec = pl.BlockSpec(memory_space=pl.ANY)
        f32 = jnp.float32
        rates = pl.pallas_call(
            functools.partial(kernel, sizes, local),
            out_shape=[pltpu.VMEM(local, f32)] * 3,
            in_specs=[any_spec] * 5,
            out_specs=[pl.BlockSpec(memory_space=pltpu.VMEM)] * 3,
            scratch_shapes=[
                pltpu.VMEM((3, size_x + 2 * REACH, size_y, size_z), f32),
                pltpu.VMEM(modes.shape, jnp.int32),
                pltpu.VMEM(late.shape, f32),
                pltpu.VMEM((rows, 4 * HALF), f32),
                pltpu.VMEM((size_z, 4 * HALF), jnp.bfloat16),
                pltpu.VMEM((size_z, 4 * HALF), jnp.bfloat16),
                pltpu.VMEM((4 * HALF, size_z), jnp.bfloat16),
                pltpu.VMEM((4 * HALF, size_z), jnp.bfloat16),
                pltpu.VMEM((2, size_x, size_y + 16, size_z), f32),
                pltpu.VMEM((2, 2, size_x, 8, size_z), f32),
                pltpu.VMEM((2, size_x, 8, size_z), f32),
                pltpu.VMEM((2, 8, rows), f32),
                pltpu.VMEM((2, 2, 8, rows), f32),
                pltpu.VMEM((1, 2 * HALF), f32),
                pltpu.VMEM((total, 1, 2 * HALF), f32),
                pltpu.VMEM((1, 2 * HALF), f32),
                pltpu.SemaphoreType.DMA((3,)),
                pltpu.SemaphoreType.DMA,
                pltpu.SemaphoreType.DMA,
                pltpu.SemaphoreType.DMA,
                pltpu.SemaphoreType.DMA,
                pltpu.SemaphoreType.REGULAR,
                pltpu.VMEM((halo_bytes // 4096, 8, 128), f32),
            ],
            compiler_params=pltpu.CompilerParams(collective_id=0, has_side_effects=True),
            name="flame",
        )(density, momentum, hydrogen, modes, jnp.asarray(late))
        return tuple(pl.pallas_call(
            write_out,
            out_shape=[jax.ShapeDtypeStruct(local, f32)] * 3,
            in_specs=[pl.BlockSpec(memory_space=pltpu.VMEM)] * 3,
            out_specs=[any_spec] * 3,
            scratch_shapes=[pltpu.SemaphoreType.DMA],
            name="write",
        )(*[pltpu.with_memory_space_constraint(r, pltpu.VMEM) for r in rates]))

    in_specs = (P("gx", "gy", "gz"), P("gx", "gy", "gz"), P("gx", "gy", "gz"), P())
    out_specs = (P("gx", "gy", "gz"), P("gx", "gy", "gz"), P("gx", "gy", "gz"))
    return jax.shard_map(
        per_device, mesh=mesh, in_specs=in_specs, out_specs=out_specs, check_vma=False
    )
```

profile of v0, /device:TPU:0, one launch (start us, length us, event | category | flops | bytes accessed | tf_op | source)
XLA Modules:
  0.0 11.1 jit_solution(8815704622207908896)
XLA Ops:
  0.6 9.8 %flame.1 = (f32[8,16,128]{2,1,0:T(8,128)S(1)}, f32[8,16,128]{2,1,0:T(8,128)S(1)}, f32[8,16,128]{2,1,0:T(8,128)S(1)}) custom-call(f32[8,16,128]{2,1,0:T(8,128)} %dens_hbm.1, f32[8,16,128]{2,1,0:T(8,128)} %mom_hbm.1, f32[8,16,128]{2,1,0:T(8,128)} %fuel_hbm.1, s32[3,96]{1,0:T(4,128)} %bitcast.1, f32[144,128]{1,0:T(8,128)} %constant.2.clone.late_hbm), custom_call_target="tpu_custom_call" | custom-call | tf_op jit(solution)/shard_map/flame/pallas_call | solution.py:422
  10.5 0.7 %write.1 = (f32[8,16,128]{2,1,0:T(8,128)}, f32[8,16,128]{2,1,0:T(8,128)}, f32[8,16,128]{2,1,0:T(8,128)}) custom-call(f32[8,16,128]{2,1,0:T(8,128)S(1)} %get-tuple-element.6.refs_0_, f32[8,16,128]{2,1,0:T(8,128)S(1)} %get-tuple-element.7.refs_1_, f32[8,16,128]{2,1,0:T(8,128)S(1)} %get-tuple-element.8.refs_2_), custom_call_target="tpu_custom_call" | custom-call | tf_op jit(solution)/shard_map/write/pallas_call | solution.py:455
where the time goes:
time: 11.3 us; the launch traced here: 11.1 us
  Pallas kernels  10.5 us (93%)
  between operations  0.64 us (6%)
    pallas_call x1, Pallas kernels, per_device(): pl.pallas_call(functools.partial(kernel, sizes, local), out_shape=[pltpu....  9.82 us
    pallas_call x1, Pallas kernels, per_device(): pl.pallas_call(write_out, out_shape=[jax.ShapeDtypeStruct(local, f32)] *...  0.68 us

commit v1 on v0

--- a/solution.py
+++ b/solution.py
@@ -134,7 +134,7 @@
 def kernel(sizes, local, dens_hbm, mom_hbm, fuel_hbm, modes_hbm, late_hbm,
            drate, mrate, hrate,
            f, modes, late, cells, along, along_low, across, across_low, edges, sides, ypack, zpack, ztile, own_sum, got_sums, full_sum,
-           load_sem, send_sem, halo_recv, z_recv, sum_recv, z_ready, measure):
+           halo_recv, z_recv, sum_recv, z_ready, measure, load_sem, send_sem):
     size_x, size_y, size_z = local
     rows = size_x * size_y
     me = {a: lax.axis_index(a) for a in sizes}
@@ -361,19 +361,19 @@
     def _():
         got = got_sums.at[pl.ds(0, total - 1)]
         pltpu.make_async_copy(got, got, sum_recv).wait()
-        full_sum[...] = tree_sum([got_sums[i] for i in range(total)])
-
-    if leaves:
-        @pl.when(rank == root_ranks[-1])
-        def _():
-            for i in reversed(leaves):
-                spread(i).start()
-
-        @pl.when(jnp.logical_not(is_root))
-        def _():
-            pltpu.make_async_copy(full_sum, full_sum, sum_recv).wait()
-
-    cube = full_sum[...]
+
+    @pl.when(jnp.logical_not(is_root))
+    def _():
+        pltpu.make_async_copy(full_sum, full_sum, sum_recv).wait()
+
+    cube = jnp.where(is_root, tree_sum([got_sums[i] for i in range(total)]), full_sum[...])
+
+    @pl.when(rank == root_ranks[-1])
+    def _():
+        full_sum[...] = cube
+        for i in reversed(leaves):
+            spread(i).start()
+
     coef = cube / ncell
     energy = jnp.sum(chosen * coef * coef, axis=1, keepdims=True)
     scale = 1.0 / (energy + ENERGY_EPS)
@@ -397,6 +397,11 @@
             pltpu.make_async_copy(sent, sent, send_sem).wait()
 
 
+def scoped_kernel(sizes, local, *refs):
+    pl.run_scoped(functools.partial(kernel, sizes, local, *refs),
+                  pltpu.SemaphoreType.DMA((3,)), pltpu.SemaphoreType.DMA)
+
+
 def write_out(*refs):
     count = len(refs) // 2
     copies = [pltpu.make_async_copy(refs[i], refs[count + i], refs[-1]) for i in range(count)]
@@ -420,7 +425,7 @@
         any_spec = pl.BlockSpec(memory_space=pl.ANY)
         f32 = jnp.float32
         rates = pl.pallas_call(
-            functools.partial(kernel, sizes, local),
+            functools.partial(scoped_kernel, sizes, local),
             out_shape=[pltpu.VMEM(local, f32)] * 3,
             in_specs=[any_spec] * 5,
             out_specs=[pl.BlockSpec(memory_space=pltpu.VMEM)] * 3,
@@ -441,8 +446,6 @@
                 pltpu.VMEM((1, 2 * HALF), f32),
                 pltpu.VMEM((total, 1, 2 * HALF), f32),
                 pltpu.VMEM((1, 2 * HALF), f32),
-                pltpu.SemaphoreType.DMA((3,)),
-                pltpu.SemaphoreType.DMA,
                 pltpu.SemaphoreType.DMA,
                 pltpu.SemaphoreType.DMA,
                 pltpu.SemaphoreType.DMA,

time: 11.3 us -> 11.2 us (level)
  no operation moved by 1% of the time
where the time goes in v1:
time: 11.2 us; the launch traced here: 11.1 us
  Pallas kernels  10.5 us (94%)
  between operations  0.64 us (6%)
    pallas_call x1, Pallas kernels, per_device(): pl.pallas_call(functools.partial(scoped_kernel, sizes, local), out_shape=...  9.78 us
    pallas_call x1, Pallas kernels, per_device(): pl.pallas_call(write_out, out_shape=[jax.ShapeDtypeStruct(local, f32)] *...  0.68 us

profile of v1, /device:TPU:0, one launch (start us, length us, event | category | flops | bytes accessed | tf_op | source)
XLA Modules:
  0.0 11.1 jit_solution(9056340505837221793)
XLA Ops:
  0.6 9.8 %flame.1 = (f32[8,16,128]{2,1,0:T(8,128)S(1)}, f32[8,16,128]{2,1,0:T(8,128)S(1)}, f32[8,16,128]{2,1,0:T(8,128)S(1)}) custom-call(f32[8,16,128]{2,1,0:T(8,128)} %refs_0_.1, f32[8,16,128]{2,1,0:T(8,128)} %refs_1_.1, f32[8,16,128]{2,1,0:T(8,128)} %refs_2_.1, s32[3,96]{1,0:T(4,128)} %bitcast.1, f32[144,128]{1,0:T(8,128)} %constant.2.clone.refs_4_), custom_call_target="tpu_custom_call" | custom-call | tf_op jit(solution)/shard_map/flame/pallas_call | solution.py:427
  10.4 0.7 %write.1 = (f32[8,16,128]{2,1,0:T(8,128)}, f32[8,16,128]{2,1,0:T(8,128)}, f32[8,16,128]{2,1,0:T(8,128)}) custom-call(f32[8,16,128]{2,1,0:T(8,128)S(1)} %get-tuple-element.6.refs_0_, f32[8,16,128]{2,1,0:T(8,128)S(1)} %get-tuple-element.7.refs_1_, f32[8,16,128]{2,1,0:T(8,128)S(1)} %get-tuple-element.8.refs_2_), custom_call_target="tpu_custom_call" | custom-call | tf_op jit(solution)/shard_map/write/pallas_call | solution.py:458

commit v2 on v1

--- a/solution.py
+++ b/solution.py
@@ -134,7 +134,7 @@
 def kernel(sizes, local, dens_hbm, mom_hbm, fuel_hbm, modes_hbm, late_hbm,
            drate, mrate, hrate,
            f, modes, late, cells, along, along_low, across, across_low, edges, sides, ypack, zpack, ztile, own_sum, got_sums, full_sum,
-           halo_recv, z_recv, sum_recv, z_ready, measure, load_sem, send_sem):
+           load_sem, send_sem, halo_recv, z_recv, sum_recv, z_ready, measure):
     size_x, size_y, size_z = local
     rows = size_x * size_y
     me = {a: lax.axis_index(a) for a in sizes}
@@ -157,13 +157,13 @@
         return {axis: lax.rem(me[axis] + step % sizes[axis], sizes[axis])}
 
     own = pl.ds(REACH, size_x)
-    load_late = pltpu.make_async_copy(late_hbm, late, load_sem.at[1])
+    load_late = pltpu.make_async_copy(late_hbm, late, load_sem)
     for at in range(0, size_x, LOAD_PLANES):
         for i, src in enumerate((dens_hbm, mom_hbm)):
             pltpu.make_async_copy(
-                src.at[pl.ds(at, LOAD_PLANES)], f.at[i, pl.ds(REACH + at, LOAD_PLANES)], load_sem.at[0]).start()
-    load_fuel = pltpu.make_async_copy(fuel_hbm, f.at[2, own], load_sem.at[1])
-    load_modes = pltpu.make_async_copy(modes_hbm, modes, load_sem.at[2])
+                src.at[pl.ds(at, LOAD_PLANES)], f.at[i, pl.ds(REACH + at, LOAD_PLANES)], load_sem).start()
+    load_fuel = pltpu.make_async_copy(fuel_hbm, f.at[2, own], load_sem)
+    load_modes = pltpu.make_async_copy(modes_hbm, modes, load_sem)
 
     barrier = pltpu.get_barrier_semaphore()
     z_steps = (1, -1)
@@ -220,11 +220,10 @@
             along[z : z + 16, 2 * HALF * i : 2 * HALF * (i + 1)] = high.astype(jnp.bfloat16)
             along_low[z : z + 16, 2 * HALF * i : 2 * HALF * (i + 1)] = rest.astype(jnp.bfloat16)
 
+    both_loaded = f.at[pl.ds(0, 2), own]
+    pltpu.make_async_copy(both_loaded, both_loaded, load_sem).wait()
     load_fuel.start()
     load_late.start()
-    load_modes.start()
-    both_loaded = f.at[pl.ds(0, 2), own]
-    pltpu.make_async_copy(both_loaded, both_loaded, load_sem.at[0]).wait()
     flat = lambda i: f[i, own].reshape(rows, size_z)
     high, rest = split(flat(1) / flat(0))
     part = dot_split(jnp.concatenate([high, rest], 1), jnp.concatenate([along[...], along[...]], 0), ((1,), (0,)))
@@ -252,7 +251,8 @@
             pl.semaphore_signal(z_ready, inc=1, device_id=shifted("gz", step), device_id_type=MESH)
 
     both_loaded = measure.at[pl.ds(0, (fuel_hbm.size + late_hbm.size) // 1024)]
-    pltpu.make_async_copy(both_loaded, both_loaded, load_sem.at[1]).wait()
+    pltpu.make_async_copy(both_loaded, both_loaded, load_sem).wait()
+    load_modes.start()
     halos_x = [
         copy_out(f.at[:, pl.ds(size_x, REACH)], f.at[:, pl.ds(0, REACH)], halo_recv, shifted("gx", 1)),
         copy_out(f.at[:, pl.ds(REACH, REACH)], f.at[:, pl.ds(size_x + REACH, REACH)], halo_recv,
@@ -397,11 +397,6 @@
             pltpu.make_async_copy(sent, sent, send_sem).wait()
 
 
-def scoped_kernel(sizes, local, *refs):
-    pl.run_scoped(functools.partial(kernel, sizes, local, *refs),
-                  pltpu.SemaphoreType.DMA((3,)), pltpu.SemaphoreType.DMA)
-
-
 def write_out(*refs):
     count = len(refs) // 2
     copies = [pltpu.make_async_copy(refs[i], refs[count + i], refs[-1]) for i in range(count)]
@@ -425,7 +420,7 @@
         any_spec = pl.BlockSpec(memory_space=pl.ANY)
         f32 = jnp.float32
         rates = pl.pallas_call(
-            functools.partial(scoped_kernel, sizes, local),
+            functools.partial(kernel, sizes, local),
             out_shape=[pltpu.VMEM(local, f32)] * 3,
             in_specs=[any_spec] * 5,
             out_specs=[pl.BlockSpec(memory_space=pltpu.VMEM)] * 3,
@@ -449,6 +444,8 @@
                 pltpu.SemaphoreType.DMA,
                 pltpu.SemaphoreType.DMA,
                 pltpu.SemaphoreType.DMA,
+                pltpu.SemaphoreType.DMA,
+                pltpu.SemaphoreType.DMA,
                 pltpu.SemaphoreType.REGULAR,
                 pltpu.VMEM((halo_bytes // 4096, 8, 128), f32),
             ],

time: 11.2 us -> 11.3 us (level)
  no operation moved by 1% of the time
where the time goes in v2:
time: 11.3 us; the launch traced here: 11.1 us
  Pallas kernels  10.5 us (93%)
  between operations  0.64 us (6%)
    pallas_call x1, Pallas kernels, per_device(): pl.pallas_call(functools.partial(kernel, sizes, local), out_shape=[pltpu....  9.8 us
    pallas_call x1, Pallas kernels, per_device(): pl.pallas_call(write_out, out_shape=[jax.ShapeDtypeStruct(local, f32)] *...  0.68 us

profile of v2, /device:TPU:0, one launch (start us, length us, event | category | flops | bytes accessed | tf_op | source)
XLA Modules:
  0.0 11.1 jit_solution(4610467676389454428)
XLA Ops:
  0.6 9.8 %flame.1 = (f32[8,16,128]{2,1,0:T(8,128)S(1)}, f32[8,16,128]{2,1,0:T(8,128)S(1)}, f32[8,16,128]{2,1,0:T(8,128)S(1)}) custom-call(f32[8,16,128]{2,1,0:T(8,128)} %dens_hbm.1, f32[8,16,128]{2,1,0:T(8,128)} %mom_hbm.1, f32[8,16,128]{2,1,0:T(8,128)} %fuel_hbm.1, s32[3,96]{1,0:T(4,128)} %bitcast.1, f32[144,128]{1,0:T(8,128)} %constant.2.clone.late_hbm), custom_call_target="tpu_custom_call" | custom-call | tf_op jit(solution)/shard_map/flame/pallas_call | solution.py:422
  10.4 0.7 %write.1 = (f32[8,16,128]{2,1,0:T(8,128)}, f32[8,16,128]{2,1,0:T(8,128)}, f32[8,16,128]{2,1,0:T(8,128)}) custom-call(f32[8,16,128]{2,1,0:T(8,128)S(1)} %get-tuple-element.6.refs_0_, f32[8,16,128]{2,1,0:T(8,128)S(1)} %get-tuple-element.7.refs_1_, f32[8,16,128]{2,1,0:T(8,128)S(1)} %get-tuple-element.8.refs_2_), custom_call_target="tpu_custom_call" | custom-call | tf_op jit(solution)/shard_map/write/pallas_call | solution.py:455

commit v3 on v2

--- a/solution.py
+++ b/solution.py
@@ -132,8 +132,8 @@
 
 
 def kernel(sizes, local, dens_hbm, mom_hbm, fuel_hbm, modes_hbm, late_hbm,
-           drate, mrate, hrate,
-           f, modes, late, cells, along, along_low, across, across_low, edges, sides, ypack, zpack, ztile, own_sum, got_sums, full_sum,
+           drate, mrate, hrate, dens_out, cells, across, across_low, chosen_out, total_out,
+           f, modes, late, along, along_low, edges, sides, ypack, zpack, ztile, own_sum, got_sums, full_sum,
            load_sem, send_sem, halo_recv, z_recv, sum_recv, z_ready, measure):
     size_x, size_y, size_z = local
     rows = size_x * size_y
@@ -297,8 +297,8 @@
     both_ways = jnp.where(used & (mine == code), 1.0, 0.0) + jnp.where(used & (mine == -code), 1.0, 0.0)
     chosen = dot_nt(jnp.ones((8, count), jnp.float32), both_ways)[0:1]
 
-    ncell = float(rows * size_z * total)
-    gain = chosen * (2.0 * FORCE_POWER / ncell)
+    chosen_out[...] = chosen
+    dens_out[...] = f[0, own]
     for i in range(2):
         here = pl.ds(2 * HALF * i, 2 * HALF)
         across[here] = along[:, here].astype(jnp.float32).T.astype(jnp.bfloat16)
@@ -374,16 +374,7 @@
         for i in reversed(leaves):
             spread(i).start()
 
-    coef = cube / ncell
-    energy = jnp.sum(chosen * coef * coef, axis=1, keepdims=True)
-    scale = 1.0 / (energy + ENERGY_EPS)
-    lit = gain * cube
-    high, rest = split(cells[...] * jnp.concatenate([lit, lit], 1))
-    both = dot_split(high, jnp.concatenate([across[...], across_low[...]], 1), ((1,), (0,)))
-    weight = flat(0) * scale
-    low = weight * (both[:, 0:size_z] + both[:, size_z:]) + weight * dot_split(rest, across[...], ((1,), (0,)))
-    mrate[...] = mrate[...] + low.reshape(size_x, size_y, size_z)
-
+    total_out[...] = cube
     for sent in (arrived[0], arrived[1], ztile.at[:, :]):
         pltpu.make_async_copy(sent, sent, send_sem).wait()
     for r in root_ranks:
@@ -397,13 +388,29 @@
             pltpu.make_async_copy(sent, sent, send_sem).wait()
 
 
-def write_out(*refs):
-    count = len(refs) // 2
-    copies = [pltpu.make_async_copy(refs[i], refs[count + i], refs[-1]) for i in range(count)]
-    for copy in copies:
+def finish(ncell, drate, mrate, hrate, dens, cells, across, across_low, chosen, total,
+           drate_hbm, mrate_hbm, hrate_hbm, result, sem):
+    size_x, size_y, size_z = dens.shape
+    rows = size_x * size_y
+    early = [pltpu.make_async_copy(drate, drate_hbm, sem), pltpu.make_async_copy(hrate, hrate_hbm, sem)]
+    for copy in early:
         copy.start()
-    for copy in copies:
+    coef = total[...] / ncell
+    energy = jnp.sum(chosen[...] * coef * coef, axis=1, keepdims=True)
+    scale = 1.0 / (energy + ENERGY_EPS)
+    lit = chosen[...] * (2.0 * FORCE_POWER / ncell) * total[...]
+    high, rest = split(cells[...] * jnp.concatenate([lit, lit], 1))
+    both = dot_split(high, jnp.concatenate([across[...], across_low[...]], 1), ((1,), (0,)))
+    weight = dens[...].reshape(rows, size_z) * scale
+    low = weight * (both[:, 0:size_z] + both[:, size_z:]) + weight * dot_split(rest, across[...], ((1,), (0,)))
+    low = low.reshape(size_x, size_y, size_z)
+    for at in range(0, size_x, size_x // 2):
+        here = pl.ds(at, size_x // 2)
+        result[here] = mrate[here] + low[at : at + size_x // 2]
+        pltpu.make_async_copy(result.at[here], mrate_hbm.at[here], sem).start()
+    for copy in early:
         copy.wait()
+    pltpu.make_async_copy(result, mrate_hbm, sem).wait()
 
 
 def solution(mesh):
@@ -421,18 +428,21 @@
         f32 = jnp.float32
         rates = pl.pallas_call(
             functools.partial(kernel, sizes, local),
-            out_shape=[pltpu.VMEM(local, f32)] * 3,
+            out_shape=[pltpu.VMEM(local, f32)] * 4 + [
+                pltpu.VMEM((rows, 4 * HALF), f32),
+                pltpu.VMEM((4 * HALF, size_z), jnp.bfloat16),
+                pltpu.VMEM((4 * HALF, size_z), jnp.bfloat16),
+                pltpu.VMEM((1, 2 * HALF), f32),
+                pltpu.VMEM((1, 2 * HALF), f32),
+            ],
             in_specs=[any_spec] * 5,
-            out_specs=[pl.BlockSpec(memory_space=pltpu.VMEM)] * 3,
+            out_specs=[pl.BlockSpec(memory_space=pltpu.VMEM)] * 9,
             scratch_shapes=[
                 pltpu.VMEM((3, size_x + 2 * REACH, size_y, size_z), f32),
                 pltpu.VMEM(modes.shape, jnp.int32),
                 pltpu.VMEM(late.shape, f32),
-                pltpu.VMEM((rows, 4 * HALF), f32),
                 pltpu.VMEM((size_z, 4 * HALF), jnp.bfloat16),
                 pltpu.VMEM((size_z, 4 * HALF), jnp.bfloat16),
-                pltpu.VMEM((4 * HALF, size_z), jnp.bfloat16),
-                pltpu.VMEM((4 * HALF, size_z), jnp.bfloat16),
                 pltpu.VMEM((2, size_x, size_y + 16, size_z), f32),
                 pltpu.VMEM((2, 2, size_x, 8, size_z), f32),
                 pltpu.VMEM((2, size_x, 8, size_z), f32),
@@ -453,11 +463,11 @@
             name="flame",
         )(density, momentum, hydrogen, modes, jnp.asarray(late))
         return tuple(pl.pallas_call(
-            write_out,
+            functools.partial(finish, float(rows * size_z * total)),
             out_shape=[jax.ShapeDtypeStruct(local, f32)] * 3,
-            in_specs=[pl.BlockSpec(memory_space=pltpu.VMEM)] * 3,
+            in_specs=[pl.BlockSpec(memory_space=pltpu.VMEM)] * 9,
             out_specs=[any_spec] * 3,
-            scratch_shapes=[pltpu.SemaphoreType.DMA],
+            scratch_shapes=[pltpu.VMEM(local, f32), pltpu.SemaphoreType.DMA],
             name="write",
         )(*[pltpu.with_memory_space_constraint(r, pltpu.VMEM) for r in rates]))
 

time: 11.3 us -> 11.3 us (level)
    pallas_call x1, Pallas kernels: 9.8 us -> 9.61 us  [per_device(): pl.pallas_call(functools.partial(kernel, sizes, local), out_shape=[pltpu....]
    pallas_call x1, Pallas kernels: 0.68 us -> 0.82 us  [per_device(): pl.pallas_call(functools.partial(finish, float(rows * size_z * total)), o...]
where the time goes in v3:
time: 11.3 us; the launch traced here: 11.1 us
  Pallas kernels  10.4 us (92%)
  between operations  0.64 us (6%)
    pallas_call x1, Pallas kernels, per_device(): pl.pallas_call(functools.partial(kernel, sizes, local), out_shape=[pltpu....  9.61 us
    pallas_call x1, Pallas kernels, per_device(): pl.pallas_call(functools.partial(finish, float(rows * size_z * total)), o...  0.82 us

profile of v3, /device:TPU:0, one launch (start us, length us, event | category | flops | bytes accessed | tf_op | source)
XLA Modules:
  0.0 11.1 jit_solution(70766501165944738)
XLA Ops:
  0.6 9.6 %flame.1 = (f32[8,16,128]{2,1,0:T(8,128)S(1)}, f32[8,16,128]{2,1,0:T(8,128)S(1)}, f32[8,16,128]{2,1,0:T(8,128)S(1)}, f32[8,16,128]{2,1,0:T(8,128)S(1)}, f32[128,...) custom-call(f32[8,16,128]{2,1,0:T(8,128)} %dens_hbm.1, ...), custom_call_target="tpu_custom_call" | custom-call | tf_op jit(solution)/shard_map/flame/pallas_call | solution.py:429
  10.2 0.8 %write.1 = (f32[8,16,128]{2,1,0:T(8,128)}, f32[8,16,128]{2,1,0:T(8,128)}, f32[8,16,128]{2,1,0:T(8,128)}) custom-call(f32[8,16,128]{2,1,0:T(8,128)S(1)} %get-tuple-element.12.drate, f32[8,16,128]{2,1,0:T(8,128)S(1)} %get-tuple-element.13.mrate, f32[8,16,128]{2,1,0:T(8,128)S(1)} %get-tuple-element.14.hrate, f32[8,16,128]{2,1,0:T(8,128)S(1)} %get-tuple-element.15.dens, ...), custom_call_target="tpu_custom_call" | custom-call | tf_op jit(solution)/shard_map/write/pallas_call | solution.py:465

commit v4 on v3

--- a/solution.py
+++ b/solution.py
@@ -404,9 +404,9 @@
     weight = dens[...].reshape(rows, size_z) * scale
     low = weight * (both[:, 0:size_z] + both[:, size_z:]) + weight * dot_split(rest, across[...], ((1,), (0,)))
     low = low.reshape(size_x, size_y, size_z)
-    for at in range(0, size_x, size_x // 2):
-        here = pl.ds(at, size_x // 2)
-        result[here] = mrate[here] + low[at : at + size_x // 2]
+    for at in range(0, size_x, size_x // 4):
+        here = pl.ds(at, size_x // 4)
+        result[here] = mrate[here] + low[at : at + size_x // 4]
         pltpu.make_async_copy(result.at[here], mrate_hbm.at[here], sem).start()
     for copy in early:
         copy.wait()

time: 11.3 us -> 11.3 us (level)
  no operation moved by 1% of the time
where the time goes in v4:
time: 11.3 us; the launch traced here: 11.1 us
  Pallas kernels  10.4 us (92%)
  between operations  0.64 us (6%)
    pallas_call x1, Pallas kernels, per_device(): pl.pallas_call(functools.partial(kernel, sizes, local), out_shape=[pltpu....  9.61 us
    pallas_call x1, Pallas kernels, per_device(): pl.pallas_call(functools.partial(finish, float(rows * size_z * total)), o...  0.81 us

profile of v4, /device:TPU:0, one launch (start us, length us, event | category | flops | bytes accessed | tf_op | source)
XLA Modules:
  0.0 11.1 jit_solution(5327438857618790782)
XLA Ops:
  0.6 9.6 %flame.1 = (f32[8,16,128]{2,1,0:T(8,128)S(1)}, f32[8,16,128]{2,1,0:T(8,128)S(1)}, f32[8,16,128]{2,1,0:T(8,128)S(1)}, f32[8,16,128]{2,1,0:T(8,128)S(1)}, f32[128,...) custom-call(f32[8,16,128]{2,1,0:T(8,128)} %dens_hbm.1, ...), custom_call_target="tpu_custom_call" | custom-call | tf_op jit(solution)/shard_map/flame/pallas_call | solution.py:429
  10.2 0.8 %write.1 = (f32[8,16,128]{2,1,0:T(8,128)}, f32[8,16,128]{2,1,0:T(8,128)}, f32[8,16,128]{2,1,0:T(8,128)}) custom-call(f32[8,16,128]{2,1,0:T(8,128)S(1)} %get-tuple-element.12.drate, f32[8,16,128]{2,1,0:T(8,128)S(1)} %get-tuple-element.13.mrate, f32[8,16,128]{2,1,0:T(8,128)S(1)} %get-tuple-element.14.hrate, f32[8,16,128]{2,1,0:T(8,128)S(1)} %get-tuple-element.15.dens, ...), custom_call_target="tpu_custom_call" | custom-call | tf_op jit(solution)/shard_map/write/pallas_call | solution.py:465

commit v5 on v4

--- a/solution.py
+++ b/solution.py
@@ -134,7 +134,7 @@
 def kernel(sizes, local, dens_hbm, mom_hbm, fuel_hbm, modes_hbm, late_hbm,
            drate, mrate, hrate, dens_out, cells, across, across_low, chosen_out, total_out,
            f, modes, late, along, along_low, edges, sides, ypack, zpack, ztile, own_sum, got_sums, full_sum,
-           load_sem, send_sem, halo_recv, z_recv, sum_recv, z_ready, measure):
+           load_sem, send_sem, halo_recv, sum_recv, z_ready, measure):
     size_x, size_y, size_z = local
     rows = size_x * size_y
     me = {a: lax.axis_index(a) for a in sizes}
@@ -274,7 +274,7 @@
     for i in range(2):
         zpack[i] = tree_sum([ends[:, (3 * i + j) * rows : (3 * i + j + 1) * rows] for j in range(3)])
     halos_y = [copy_out(ypack, sides.at[i], halo_recv, shifted("gy", step)) for i, step in enumerate(y_steps)]
-    halos_z = [copy_out(zpack, ztile.at[i], z_recv, shifted("gz", step)) for i, step in enumerate(z_steps)]
+    halos_z = [copy_out(zpack, ztile.at[i], halo_recv, shifted("gz", step)) for i, step in enumerate(z_steps)]
     for copy, lower in zip(halos_z, z_lower):
         @pl.when(lower)
         def _(copy=copy):
@@ -350,7 +350,6 @@
                   - mid_fuel * jnp.exp(-ACTIVATION * mid_fuel / planes(dens, 0)))
     mrate[...] = VISCOSITY * (mrate[...] + second_diff(mom)) - first_diff(mom * vel_pad + dens)
 
-    pltpu.make_async_copy(ztile, ztile, z_recv).wait()
     for i, rate in enumerate((VISCOSITY, DIFFUSIVITY)):
         tile = jnp.concatenate([ztile[0, i], ztile[1, i]], 0)
         outs[1 + i][...] = outs[1 + i][...] + rate * dot_tn(tile, late[0:16]).reshape(size_x, size_y, size_z)
@@ -423,7 +422,7 @@
         late = tables(size_z)
         modes = forced_modes.T
         total = math.prod(sizes.values())
-        halo_bytes = 4 * (3 * 2 * REACH * size_y + (1 + (sizes["gy"] > 2)) * 2 * size_x * 8) * size_z
+        halo_bytes = 4 * (3 * 2 * REACH * size_y + (1 + (sizes["gy"] > 2)) * 2 * size_x * 8) * size_z + 4 * 2 * 2 * 8 * rows
         any_spec = pl.BlockSpec(memory_space=pl.ANY)
         f32 = jnp.float32
         rates = pl.pallas_call(
@@ -455,7 +454,6 @@
                 pltpu.SemaphoreType.DMA,
                 pltpu.SemaphoreType.DMA,
                 pltpu.SemaphoreType.DMA,
-                pltpu.SemaphoreType.DMA,
                 pltpu.SemaphoreType.REGULAR,
                 pltpu.VMEM((halo_bytes // 4096, 8, 128), f32),
             ],

time: 11.3 us -> 11.3 us (level)
  no operation moved by 1% of the time
where the time goes in v5:
time: 11.3 us; the launch traced here: 11 us
  Pallas kernels  10.4 us (92%)
  between operations  0.64 us (6%)
    pallas_call x1, Pallas kernels, per_device(): pl.pallas_call(functools.partial(kernel, sizes, local), out_shape=[pltpu....  9.6 us
    pallas_call x1, Pallas kernels, per_device(): pl.pallas_call(functools.partial(finish, float(rows * size_z * total)), o...  0.81 us

profile of v5, /device:TPU:0, one launch (start us, length us, event | category | flops | bytes accessed | tf_op | source)
XLA Modules:
  0.0 11.0 jit_solution(6140588142516677086)
XLA Ops:
  0.6 9.6 %flame.1 = (f32[8,16,128]{2,1,0:T(8,128)S(1)}, f32[8,16,128]{2,1,0:T(8,128)S(1)}, f32[8,16,128]{2,1,0:T(8,128)S(1)}, f32[8,16,128]{2,1,0:T(8,128)S(1)}, f32[128,...) custom-call(f32[8,16,128]{2,1,0:T(8,128)} %dens_hbm.1, ...), custom_call_target="tpu_custom_call" | custom-call | tf_op jit(solution)/shard_map/flame/pallas_call | solution.py:428
  10.2 0.8 %write.1 = (f32[8,16,128]{2,1,0:T(8,128)}, f32[8,16,128]{2,1,0:T(8,128)}, f32[8,16,128]{2,1,0:T(8,128)}) custom-call(f32[8,16,128]{2,1,0:T(8,128)S(1)} %get-tuple-element.12.drate, f32[8,16,128]{2,1,0:T(8,128)S(1)} %get-tuple-element.13.mrate, f32[8,16,128]{2,1,0:T(8,128)S(1)} %get-tuple-element.14.hrate, f32[8,16,128]{2,1,0:T(8,128)S(1)} %get-tuple-element.15.dens, ...), custom_call_target="tpu_custom_call" | custom-call | tf_op jit(solution)/shard_map/write/pallas_call | solution.py:463
